TPU v7x, 32 devices: a whole 2x2x4 slice. The times are simulated.
32 devices in a mesh: com: 8 (over y, x, core), arc: 4 (over z).
Axes of the slice: x: 2, y: 2, z: 4, core: 2. Of those that a mesh axis runs over, the one named last changes fastest.
Arguments:
- flow_start: float32 [256, 65536], P('com', 'arc'), may hold values from 0 to 1
- price_start: float32 [256, 16384], P('com'), may hold values from -3 to 3
- cost: float32 [256, 65536], P('com', 'arc'), may hold values from -6 to 6
- demand: float32 [256, 16384], P('com'), may hold values from -6 to 6
- head_block: int32 [512], P('arc'), may hold values from 0 to 127
- tail_block: int32 [512], P('arc'), may hold values from 0 to 127
- head_local: int32 [65536], P('arc'), may hold values from 0 to 127
- tail_local: int32 [65536], P('arc'), may hold values from 0 to 127
- cap_class: int32 [65536], P('arc'), may hold values from 0 to 7
- cap_levels: float32 [8], replicated, may hold values from 25 to 128
Outputs:
- flow: float32 [256, 65536], P('com', 'arc')
- price: float32 [256, 16384], P('com')
Inputs may be any that keep to these rules, and one draw needn't show every extreme that they name: `head_block`: node block indices. `tail_block`: node block indices. `head_local`: positions within a node block. `tail_local`: positions within a node block.
All inputs are finite; a program needn't handle non-finite values.
Results may differ from a plain program's by a relative error of at most 0.00016.
Values sent between devices are 32-bit elements; how exact they have to be, the bound alone decides.
A program may use at most 128 MiB of HBM per device.

v0:
```python
import jax
import jax.numpy as jnp
from jax import lax
from jax.sharding import PartitionSpec as P

NODES = 16384
BLOCK = 128
CLASSES = 8
ITERS = 4
NEWTON = 3
step_primal = 0.25
step_dual = 0.1
soft_width = 0.05
highest = lax.Precision.HIGHEST


def column_sums(values, theta):
    excess = jnp.maximum(values - theta, 0.0)
    return (jnp.sum(excess, axis=0), jnp.sum(jnp.minimum(excess / soft_width, 1.0), axis=0))


def theta_step(theta, total, active, capacity):
    return theta + jnp.maximum(total - capacity, 0.0) / jnp.maximum(active, 1.0)


def on_device(
    flow_start,
    price_start,
    cost,
    demand,
    head_block,
    tail_block,
    head_local,
    tail_local,
    cap_class,
    cap_levels,
):
    com_rows, arc_cols = flow_start.shape
    blocks = arc_cols // BLOCK
    node_blocks = NODES // BLOCK
    lanes = jnp.arange(BLOCK, dtype=jnp.int32)
    head_table = (head_local.reshape(blocks, BLOCK)[:, :, None] == lanes).astype(jnp.float32)
    tail_table = (tail_local.reshape(blocks, BLOCK)[:, :, None] == lanes).astype(jnp.float32)
    block_ids = jnp.arange(node_blocks, dtype=jnp.int32)
    head_owner = (head_block[:, None] == block_ids).astype(jnp.float32)
    tail_owner = (tail_block[:, None] == block_ids).astype(jnp.float32)
    class_ids = jnp.arange(CLASSES, dtype=jnp.int32)
    capacity = jnp.sum(
        jnp.where(cap_class[:, None] == class_ids, cap_levels[None, :], 0.0), axis=1
    ).reshape(blocks, BLOCK)
    flow = flow_start.reshape(com_rows, blocks, BLOCK)
    unit_cost = cost.reshape(com_rows, blocks, BLOCK)
    price = price_start
    for step in range(ITERS):
        grid = price.reshape(com_rows, node_blocks, BLOCK)
        at_head = jnp.einsum("jn,knl->jkl", head_owner, grid, precision=highest)
        at_head = jnp.einsum("jkl,jal->kja", at_head, head_table, precision=highest)
        at_tail = jnp.einsum("jn,knl->jkl", tail_owner, grid, precision=highest)
        at_tail = jnp.einsum("jkl,jal->kja", at_tail, tail_table, precision=highest)
        trial = flow - step_primal * (unit_cost - (at_head - at_tail))
        values = lax.all_to_all(trial, "com", split_axis=1, concat_axis=0, tiled=True)
        limits = lax.all_to_all(capacity[None], "com", split_axis=1, concat_axis=0, tiled=True)
        theta = jnp.zeros(values.shape[1:], jnp.float32)
        for inner in range(NEWTON):
            total, active = column_sums(values, theta)
            theta = theta_step(theta, total, active, limits[0])
        fresh = lax.all_to_all(
            jnp.maximum(values - theta, 0.0), "com", split_axis=0, concat_axis=1, tiled=True
        )
        flows = 2.0 * fresh - flow
        inward = jnp.einsum("kja,jal->jkl", flows, head_table, precision=highest)
        inward = jnp.einsum("jn,jkl->knl", head_owner, inward, precision=highest)
        outward = jnp.einsum("kja,jal->jkl", flows, tail_table, precision=highest)
        outward = jnp.einsum("jn,jkl->knl", tail_owner, outward, precision=highest)
        balance = (inward - outward).reshape(com_rows, NODES)
        summed = lax.psum(balance, "arc")
        price = price + step_dual * (demand - summed)
        flow = fresh
    return (flow.reshape(com_rows, arc_cols), price)


def solution(mesh):
    return jax.shard_map(
        on_device,
        mesh=mesh,
        in_specs=(
            P("com", "arc"),
            P("com", None),
            P("com", "arc"),
            P("com", None),
            P("arc"),
            P("arc"),
            P("arc"),
            P("arc"),
            P("arc"),
            P(),
        ),
        out_specs=(P("com", "arc"), P("com", None)),
        check_vma=False,
    )
```

profile of v0, /device:TPU:0, one launch (start us, length us, event | category | flops | bytes accessed | tf_op | source)
XLA Modules:
  0.0 859.6 jit_solution(16881110937198093419)
XLA Ops:
  11.9 9.8 %fusion.7 = f32[128,128,32]{1,2,0:T(8,128)S(1)} fusion(s32[128,128]{1,0:T(8,128)S(1)} %bitcast.332, f32[128,32,128]{2,0,1:T(8,128)S(1)} %fusion.132), kind=kOutput, calls=%fused_computation.8 | convolution fusion | flops 807403520 | bytes 4259840 | tf_op jit(solution)/shard_map/jkl,jal->kja/dot_general | solution.py:59
  21.8 9.1 %fusion.33 = f32[32,128,128]{2,0,1:T(8,128)} fusion(f32[128,128,32]{1,2,0:T(8,128)S(1)} %fusion.7, f32[128,32,128]{2,0,1:T(8,128)S(1)} %fusion.119, s32[128,128]{1,0:T(8,128)S(1)} %bitcast.323, f32[32,16384]{1,0:T(8,128)S(1)} %copy-done, f32[32,16384]{1,0:T(8,128)S(1)} %copy-done.9), kind=kOutput, calls=%fused_computation.44 | convolution fusion | flops 809500672 | bytes 10551296 | tf_op jit(solution)/shard_map/jkl,jal->kja/dot_general | solution.py:57
  30.9 5.3 all-to-all-start
  37.1 25.8 %all-to-all-done = f32[32,128,128]{2,0,1:T(8,128)} async-done(((f32[32,128,128]{2,0,1:T(8,128)}), f32[32,128,128]{2,0,1:T(8,128)}, u32[]{:S(2)}, u32[]{:S(2)}) %all-to-all-start) | async-done | bytes 2097184 | tf_op jit(solution)/shard_map/all_to_all | solution.py:61
  62.9 3.4 all-to-all-start.1
  66.3 3.1 fusion.78
  69.4 4.1 copy.105
  73.5 3.2 fusion.82
  76.8 3.1 fusion.83
  80.1 30.6 %all_to_all.168 = f32[256,16,128]{2,1,0:T(8,128)S(1)} all-to-all(f32[256,16,128]{2,1,0:T(8,128)S(1)} %fusion.43), channel_id=1, replica_groups=mesh['com'=8,'arc'=4] {'com'}, dimensions={0} | all-to-all | bytes 4194304 | tf_op jit(solution)/shard_map/all_to_all | solution.py:67
  113.6 7.4 fusion.6
  121.0 7.5 fusion.14
  131.1 4.0 subtract_bitcast_fusion.3
  135.1 2.9 copy.110
  138.0 4.1 copy.234
  142.5 86.0 %all-reduce.5.cloned.1.call-done = f32[32,16384]{1,0:T(8,128)} async-done(((f32[32,16384]{1,0:T(8,128)}), f32[32,16384]{1,0:T(8,128)}) %all-reduce.5.cloned.1.call-update) | async-done | bytes 2097168 | tf_op jit(solution)/shard_map/psum | solution.py:76
  228.4 3.1 fusion.106
  234.5 9.8 %fusion.5 = f32[128,128,32]{1,2,0:T(8,128)S(1)} fusion(s32[128,128]{1,0:T(8,128)S(1)} %bitcast.334, f32[128,32,128]{2,0,1:T(8,128)S(1)} %fusion.129), kind=kOutput, calls=%fused_computation.6 | convolution fusion | flops 807403520 | bytes 4259840 | tf_op jit(solution)/shard_map/jkl,jal->kja/dot_general | solution.py:59
  244.3 10.2 %fusion.35 = f32[32,128,128]{2,0,1:T(8,128)S(1)} fusion(f32[32,8,16,128]{3,0,2,1:T(8,128)S(1)} %copy-done.6, f32[128,128,32]{1,2,0:T(8,128)S(1)} %fusion.5, f32[128,32,128]{2,0,1:T(8,128)S(1)} %fusion.116, s32[128,128]{1,0:T(8,128)S(1)} %bitcast.325, f32[32,16384]{1,0:T(8,128)S(1)} %copy-done), kind=kOutput, calls=%fused_computation.46 | convolution fusion | flops 809500672 | bytes 10551296 | tf_op jit(solution)/shard_map/jkl,jal->kja/dot_general | solution.py:57
  254.5 30.0 %all_to_all.169 = f32[32,128,128]{2,0,1:T(8,128)S(1)} all-to-all(f32[32,128,128]{2,0,1:T(8,128)S(1)} %fusion.35), channel_id=1, replica_groups=mesh['com'=8,'arc'=4] {'com'}, dimensions={1} | all-to-all | bytes 4194304 | tf_op jit(solution)/shard_map/all_to_all | solution.py:61
  290.8 29.4 %all_to_all.170 = f32[256,16,128]{2,1,0:T(8,128)S(1)} all-to-all(f32[256,16,128]{2,1,0:T(8,128)S(1)} %fusion.42), channel_id=1, replica_groups=mesh['com'=8,'arc'=4] {'com'}, dimensions={0} | all-to-all | bytes 4194304 | tf_op jit(solution)/shard_map/all_to_all | solution.py:67
  322.2 7.4 fusion.4
  329.6 7.5 fusion.12
  339.7 4.0 subtract_bitcast_fusion.2
  346.6 4.1 copy.233
  351.0 83.3 %all-reduce.7.cloned.1.call-done = f32[32,16384]{1,0:T(8,128)} async-done(((f32[32,16384]{1,0:T(8,128)}), f32[32,16384]{1,0:T(8,128)}) %all-reduce.7.cloned.1.call-update) | async-done | bytes 2097168 | tf_op jit(solution)/shard_map/psum | solution.py:76
  434.3 3.9 multiply_add_fusion.2
  442.1 9.8 %fusion.3 = f32[128,128,32]{1,2,0:T(8,128)S(1)} fusion(s32[128,128]{1,0:T(8,128)S(1)} %bitcast.336, f32[128,32,128]{2,0,1:T(8,128)S(1)} %fusion.126), kind=kOutput, calls=%fused_computation.4 | convolution fusion | flops 807403520 | bytes 4259840 | tf_op jit(solution)/shard_map/jkl,jal->kja/dot_general | solution.py:59
  451.9 10.2 %fusion.37 = f32[32,128,128]{2,0,1:T(8,128)S(1)} fusion(f32[32,8,16,128]{3,0,2,1:T(8,128)S(1)} %copy-done.4, f32[128,128,32]{1,2,0:T(8,128)S(1)} %fusion.3, f32[128,32,128]{2,0,1:T(8,128)S(1)} %fusion.113, s32[128,128]{1,0:T(8,128)S(1)} %bitcast.327, f32[32,16384]{1,0:T(8,128)S(1)} %copy-done), kind=kOutput, calls=%fused_computation.48 | convolution fusion | flops 809500672 | bytes 10551296 | tf_op jit(solution)/shard_map/jkl,jal->kja/dot_general | solution.py:57
  462.1 30.0 %all_to_all.171 = f32[32,128,128]{2,0,1:T(8,128)S(1)} all-to-all(f32[32,128,128]{2,0,1:T(8,128)S(1)} %fusion.37), channel_id=1, replica_groups=mesh['com'=8,'arc'=4] {'com'}, dimensions={1} | all-to-all | bytes 4194304 | tf_op jit(solution)/shard_map/all_to_all | solution.py:61
  498.4 29.2 %all_to_all.172 = f32[256,16,128]{2,1,0:T(8,128)S(1)} all-to-all(f32[256,16,128]{2,1,0:T(8,128)S(1)} %fusion.41), channel_id=1, replica_groups=mesh['com'=8,'arc'=4] {'com'}, dimensions={0} | all-to-all | bytes 4194304 | tf_op jit(solution)/shard_map/all_to_all | solution.py:67
  529.6 7.4 fusion.2
  537.0 7.5 fusion.10
  547.1 4.0 subtract_bitcast_fusion.1
  554.0 4.1 copy.232
  558.6 83.1 %all-reduce.9.cloned.1.call-done = f32[32,16384]{1,0:T(8,128)} async-done(((f32[32,16384]{1,0:T(8,128)}), f32[32,16384]{1,0:T(8,128)}) %all-reduce.9.cloned.1.call-update) | async-done | bytes 2097168 | tf_op jit(solution)/shard_map/psum | solution.py:76
  641.7 3.1 fusion.107
  647.7 9.8 %fusion.1 = f32[128,128,32]{1,2,0:T(8,128)S(1)} fusion(s32[128,128]{1,0:T(8,128)S(1)} %bitcast.338, f32[128,32,128]{2,0,1:T(8,128)S(1)} %fusion.123), kind=kOutput, calls=%fused_computation.2 | convolution fusion | flops 807403520 | bytes 4259840 | tf_op jit(solution)/shard_map/jkl,jal->kja/dot_general | solution.py:59
  657.6 10.2 %fusion.39 = f32[32,128,128]{2,0,1:T(8,128)S(1)} fusion(f32[32,8,16,128]{3,0,2,1:T(8,128)S(1)} %copy-done.2, f32[128,128,32]{1,2,0:T(8,128)S(1)} %fusion.1, f32[128,32,128]{2,0,1:T(8,128)S(1)} %fusion.110, s32[128,128]{1,0:T(8,128)S(1)} %bitcast.329, f32[32,16384]{1,0:T(8,128)S(1)} %copy-done), kind=kOutput, calls=%fused_computation.50 | convolution fusion | flops 809500672 | bytes 10551296 | tf_op jit(solution)/shard_map/jkl,jal->kja/dot_general | solution.py:57
  667.8 30.0 %all_to_all.173 = f32[32,128,128]{2,0,1:T(8,128)S(1)} all-to-all(f32[32,128,128]{2,0,1:T(8,128)S(1)} %fusion.39), channel_id=1, replica_groups=mesh['com'=8,'arc'=4] {'com'}, dimensions={1} | all-to-all | bytes 4194304 | tf_op jit(solution)/shard_map/all_to_all | solution.py:61
  704.1 29.2 %all_to_all.174 = f32[256,16,128]{2,1,0:T(8,128)S(1)} all-to-all(f32[256,16,128]{2,1,0:T(8,128)S(1)} %fusion.40), channel_id=1, replica_groups=mesh['com'=8,'arc'=4] {'com'}, dimensions={0} | all-to-all | bytes 4194304 | tf_op jit(solution)/shard_map/all_to_all | solution.py:67
  735.5 7.5 fusion
  743.0 7.5 fusion.8
  753.1 4.0 subtract_bitcast_fusion
  757.1 2.9 copy.135
  760.0 4.2 copy.230
  768.5 79.2 %all-reduce.11.cloned.1.call-done = f32[32,16384]{1,0:T(8,128)} async-done(((f32[32,16384]{1,0:T(8,128)}), f32[32,16384]{1,0:T(8,128)}) %all-reduce.11.cloned.1.call-update) | async-done | bytes 2097168 | tf_op jit(solution)/shard_map/psum | solution.py:76
  847.7 5.2 multiply_add_fusion
  (103 shorter events, 64.8 us)
Async XLA Ops:
  7.2 14.6 %copy-start = (f32[32,16384]{1,0:T(8,128)S(1)}, f32[32,16384]{1,0:T(8,128)}, u32[]{:S(2)}) copy-start(f32[32,16384]{1,0:T(8,128)} %param.12) | copy-start | bytes 6291460
  7.2 2.1 copy-start.15
  9.3 1.3 copy-start.16
  10.6 1.3 copy-start.13
  11.9 9.9 %copy-start.9 = (f32[32,16384]{1,0:T(8,128)S(1)}, f32[32,16384]{1,0:T(8,128)}, u32[]{:S(2)}) copy-start(f32[32,16384]{1,0:T(8,128)} %param.10) | copy-start | bytes 6291460
  11.9 9.9 %copy-start.12 = (s32[16384]{0:T(1024)S(1)}, s32[16384]{0:T(1024)}, u32[]{:S(2)}) copy-start(s32[16384]{0:T(1024)} %param.16) | copy-start | bytes 196612
  30.9 5.3 copy-start.14
  30.9 5.3 copy-start.17
  30.9 32.0 %all-to-all-start = ((f32[32,128,128]{2,0,1:T(8,128)}), f32[32,128,128]{2,0,1:T(8,128)}, u32[]{:S(2)}, u32[]{:S(2)}) async-start(f32[32,128,128]{2,0,1:T(8,128)} %fusion.33), calls=%async_computation | async-start | bytes 4194304 | tf_op jit(solution)/shard_map/all_to_all | solution.py:61
  62.9 10.6 %all-to-all-start.1 = ((f32[1,128,128]{2,0,1:T(1,128)}), f32[1,128,128]{2,0,1:T(1,128)S(1)}, u32[]{:S(2)}, u32[]{:S(2)}) async-start(f32[1,128,128]{2,0,1:T(1,128)} %bitcast.8), calls=%async_computation.1 | async-start | bytes 131072 | tf_op jit(solution)/shard_map/all_to_all | solution.py:62
  66.3 162.1 %all-reduce.5.cloned.1.call-start = ((), (), s32[]{:S(2)}) async-start(), calls=%async_computation.9 | async-start | bytes 4194304 | tf_op jit(solution)/shard_map/psum | solution.py:76
  73.5 6.4 copy-start.11
  110.7 1.6 copy-start.10
  112.3 1.3 copy-start.5
  142.2 292.1 %all-reduce.7.cloned.1.call-start = ((), (), s32[]{:S(2)}) async-start(), calls=%async_computation.10 | async-start | bytes 4194304 | tf_op jit(solution)/shard_map/psum | solution.py:76
  234.5 9.9 %copy-start.6 = (f32[32,8,16,128]{3,0,2,1:T(8,128)S(1)}, f32[32,8,16,128]{3,0,2,1:T(8,128)}, u32[]{:S(2)}) copy-start(f32[32,8,16,128]{3,0,2,1:T(8,128)} %copy-done.5) | copy-start | bytes 6291460
  320.9 1.3 copy-start.3
  350.7 290.9 %all-reduce.9.cloned.1.call-start = ((), (), s32[]{:S(2)}) async-start(), calls=%async_computation.11 | async-start | bytes 4194304 | tf_op jit(solution)/shard_map/psum | solution.py:76
  438.2 1.4 copy-start.7
  442.1 9.9 %copy-start.4 = (f32[32,8,16,128]{3,0,2,1:T(8,128)S(1)}, f32[32,8,16,128]{3,0,2,1:T(8,128)}, u32[]{:S(2)}) copy-start(f32[32,8,16,128]{3,0,2,1:T(8,128)} %copy-done.3) | copy-start | bytes 6291460
  528.3 1.3 copy-start.1
  558.1 289.5 %all-reduce.11.cloned.1.call-start = ((), (), s32[]{:S(2)}) async-start(), calls=%async_computation.12 | async-start | bytes 4194304 | tf_op jit(solution)/shard_map/psum | solution.py:76
  647.7 9.9 %copy-start.2 = (f32[32,8,16,128]{3,0,2,1:T(8,128)S(1)}, f32[32,8,16,128]{3,0,2,1:T(8,128)}, u32[]{:S(2)}) copy-start(f32[32,8,16,128]{3,0,2,1:T(8,128)} %copy-done.1) | copy-start | bytes 6291460
  733.3 1.3 copy-start.8
Sparse Core Ops, SparseCore 0:
  142.3 86.0 all-reduce.4
  350.9 83.3 all-reduce.6
  558.3 83.3 all-reduce.8
  764.3 83.3 all-reduce.10
where the time goes:
time: 868 us; the launch traced here: 860 us
  waiting for transfers between devices  357 us (41%)
  blocking collectives  209 us (24%)
  matrix products  175 us (20%)
  local copies, waits for them, and re-layouts  51.7 us (6%)
  other arithmetic  42.8 us (5%)
  between operations  14.6 us (2%)
  starting transfers between devices  9.63 us (1%)
    psum x4, waiting for transfers between devices, on_device(): summed = lax.psum(balance, 'arc')  332 us
    all_to_all x4, blocking collectives, on_device(): lax.all_to_all(jnp.maximum(values - theta, 0.0), 'com', split_axis=0, con...  118 us
    all_to_all x3, blocking collectives, on_device(): lax.all_to_all(trial, 'com', split_axis=1, concat_axis=0, tiled=True)  90 us
    dot_general x4, matrix products, on_device(): at_head = jnp.einsum('jkl,jal->kja', at_head, head_table, precision=highest)  39.7 us
    dot_general x4, matrix products, on_device(): at_tail = jnp.einsum('jkl,jal->kja', at_tail, tail_table, precision=highest)  39.3 us
    dot_general x4, matrix products, on_device(): inward = jnp.einsum('kja,jal->jkl', flows, head_table, precision=highest)  29.9 us
    dot_general x4, matrix products, on_device(): outward = jnp.einsum('kja,jal->jkl', flows, tail_table, precision=highest)  29.7 us
    unnamed x45, local copies, waits for them, and re-layouts  28 us
  transfers between devices with their start and end apart: 6, of which 5 were waited for; matrix products, arithmetic and copies ran while one was open for 1% of the time, Pallas kernels for 0%

commit v1 on v0

--- a/solution.py
+++ b/solution.py
@@ -73,7 +73,7 @@
         outward = jnp.einsum("kja,jal->jkl", flows, tail_table, precision=highest)
         outward = jnp.einsum("jn,jkl->knl", tail_owner, outward, precision=highest)
         balance = (inward - outward).reshape(com_rows, NODES)
-        summed = lax.psum(balance, "arc")
+        summed = jnp.sum(lax.all_gather(balance, "arc"), axis=0)
         price = price + step_dual * (demand - summed)
         flow = fresh
     return (flow.reshape(com_rows, arc_cols), price)

time: 868 us -> 1140 us (1.31)
  waiting for transfers between devices: 357 us -> 609 us
  other arithmetic: 42.8 us -> 64.6 us
    all_gather x0 -> x4, waiting for transfers between devices: none -> 583 us  [on_device(): summed = jnp.sum(lax.all_gather(balance, 'arc'), axis=0)]
    psum x4 -> x0, waiting for transfers between devices: 332 us -> none  [on_device(): summed = lax.psum(balance, 'arc')]
    reduce_sum x0 -> x4, other arithmetic: none -> 21.8 us  [on_device(): summed = jnp.sum(lax.all_gather(balance, 'arc'), axis=0)]
    unnamed x45 -> x41, local copies, waits for them, and re-layouts: 28 us -> 11.5 us
where the time goes in v1:
time: 1140 us; the launch traced here: 1130 us
  waiting for transfers between devices  609 us (53%)
  blocking collectives  209 us (18%)
  matrix products  175 us (15%)
  other arithmetic  64.6 us (6%)
  local copies, waits for them, and re-layouts  46.3 us (4%)
  between operations  14.6 us (1%)
    all_gather x4, waiting for transfers between devices, on_device(): summed = jnp.sum(lax.all_gather(balance, 'arc'), axis=0)  583 us
    all_to_all x4, blocking collectives, on_device(): lax.all_to_all(jnp.maximum(values - theta, 0.0), 'com', split_axis=0, con...  118 us
    all_to_all x3, blocking collectives, on_device(): lax.all_to_all(trial, 'com', split_axis=1, concat_axis=0, tiled=True)  90 us
    dot_general x4, matrix products, on_device(): at_head = jnp.einsum('jkl,jal->kja', at_head, head_table, precision=highest)  39.7 us
    dot_general x4, matrix products, on_device(): at_tail = jnp.einsum('jkl,jal->kja', at_tail, tail_table, precision=highest)  39.3 us
    dot_general x4, matrix products, on_device(): inward = jnp.einsum('kja,jal->jkl', flows, head_table, precision=highest)  29.9 us
    dot_general x4, matrix products, on_device(): outward = jnp.einsum('kja,jal->jkl', flows, tail_table, precision=highest)  29.7 us
    all_to_all x1, waiting for transfers between devices, on_device(): lax.all_to_all(trial, 'com', split_axis=1, concat_axis=0, tiled=True)  25.8 us
  transfers between devices with their start and end apart: 6, of which 5 were waited for; matrix products, arithmetic and copies ran while one was open for 1% of the time, Pallas kernels for 0%

profile of v1, /device:TPU:0, one launch (start us, length us, event | category | flops | bytes accessed | tf_op | source)
XLA Modules:
  0.0 1127.4 jit_solution(321184487123679391)
XLA Ops:
  11.9 9.8 fusion.7
  21.8 9.1 fusion.33
  30.9 5.3 all-to-all-start
  37.1 25.8 %all-to-all-done = f32[32,128,128]{2,0,1:T(8,128)} async-done(((f32[32,128,128]{2,0,1:T(8,128)}), f32[32,128,128]{2,0,1:T(8,128)}, u32[]{:S(2)}, u32[]{:S(2)}) %all-to-all-start) | async-done | bytes 2097184 | tf_op jit(solution)/shard_map/all_to_all | solution.py:61
  62.9 3.4 all-to-all-start.1
  66.3 3.1 fusion.78
  69.4 4.1 copy.105
  73.5 3.2 fusion.82
  76.8 3.1 fusion.83
  80.1 30.6 %all_to_all.168 = f32[256,16,128]{2,1,0:T(8,128)S(1)} all-to-all(f32[256,16,128]{2,1,0:T(8,128)S(1)} %fusion.43), channel_id=1, replica_groups=mesh['com'=8,'arc'=4] {'com'}, dimensions={0} | all-to-all | bytes 4194304 | tf_op jit(solution)/shard_map/all_to_all | solution.py:67
  113.6 7.4 fusion.6
  121.0 7.5 fusion.14
  131.1 4.0 subtract_bitcast_fusion.3
  135.1 2.9 copy.110
  141.1 149.4 %all-gather.5.cloned.1.call-done = f32[4,32,16384]{2,1,0:T(8,128)} async-done(((f32[1,32,16384]{2,1,0:T(8,128)}), f32[4,32,16384]{2,1,0:T(8,128)}) %all-gather.5.cloned.1.call-update) | async-done | bytes 8388624 | tf_op jit(solution)/shard_map/all_gather | solution.py:76
  290.5 5.4 reduce_sum.268
  295.9 3.1 fusion.106
  302.0 9.8 fusion.5
  311.8 10.2 fusion.35
  322.0 30.0 %all_to_all.169 = f32[32,128,128]{2,0,1:T(8,128)S(1)} all-to-all(f32[32,128,128]{2,0,1:T(8,128)S(1)} %fusion.35), channel_id=1, replica_groups=mesh['com'=8,'arc'=4] {'com'}, dimensions={1} | all-to-all | bytes 4194304 | tf_op jit(solution)/shard_map/all_to_all | solution.py:61
  358.3 29.4 %all_to_all.170 = f32[256,16,128]{2,1,0:T(8,128)S(1)} all-to-all(f32[256,16,128]{2,1,0:T(8,128)S(1)} %fusion.42), channel_id=1, replica_groups=mesh['com'=8,'arc'=4] {'com'}, dimensions={0} | all-to-all | bytes 4194304 | tf_op jit(solution)/shard_map/all_to_all | solution.py:67
  389.7 7.4 fusion.4
  397.1 7.5 fusion.12
  407.2 3.9 subtract_bitcast_fusion.2
  411.2 2.9 copy.118
  417.2 145.9 %all-gather.7.cloned.1.call-done = f32[4,32,16384]{2,1,0:T(8,128)} async-done(((f32[1,32,16384]{2,1,0:T(8,128)}), f32[4,32,16384]{2,1,0:T(8,128)}) %all-gather.7.cloned.1.call-update) | async-done | bytes 8388624 | tf_op jit(solution)/shard_map/all_gather | solution.py:76
  563.1 5.5 reduce_sum.275
  568.6 3.9 multiply_add_fusion.2
  576.5 9.8 fusion.3
  586.3 10.2 fusion.37
  596.5 30.0 %all_to_all.171 = f32[32,128,128]{2,0,1:T(8,128)S(1)} all-to-all(f32[32,128,128]{2,0,1:T(8,128)S(1)} %fusion.37), channel_id=1, replica_groups=mesh['com'=8,'arc'=4] {'com'}, dimensions={1} | all-to-all | bytes 4194304 | tf_op jit(solution)/shard_map/all_to_all | solution.py:61
  632.8 29.2 %all_to_all.172 = f32[256,16,128]{2,1,0:T(8,128)S(1)} all-to-all(f32[256,16,128]{2,1,0:T(8,128)S(1)} %fusion.41), channel_id=1, replica_groups=mesh['com'=8,'arc'=4] {'com'}, dimensions={0} | all-to-all | bytes 4194304 | tf_op jit(solution)/shard_map/all_to_all | solution.py:67
  664.0 7.4 fusion.2
  671.4 7.5 fusion.10
  681.5 4.0 subtract_bitcast_fusion.1
  691.7 145.7 %all-gather.9.cloned.1.call-done = f32[4,32,16384]{2,1,0:T(8,128)} async-done(((f32[1,32,16384]{2,1,0:T(8,128)}), f32[4,32,16384]{2,1,0:T(8,128)}) %all-gather.9.cloned.1.call-update) | async-done | bytes 8388624 | tf_op jit(solution)/shard_map/all_gather | solution.py:76
  837.3 5.4 reduce_sum.282
  842.8 3.1 fusion.107
  848.8 9.8 fusion.1
  858.7 10.2 fusion.39
  868.9 30.0 %all_to_all.173 = f32[32,128,128]{2,0,1:T(8,128)S(1)} all-to-all(f32[32,128,128]{2,0,1:T(8,128)S(1)} %fusion.39), channel_id=1, replica_groups=mesh['com'=8,'arc'=4] {'com'}, dimensions={1} | all-to-all | bytes 4194304 | tf_op jit(solution)/shard_map/all_to_all | solution.py:61
  905.2 29.2 %all_to_all.174 = f32[256,16,128]{2,1,0:T(8,128)S(1)} all-to-all(f32[256,16,128]{2,1,0:T(8,128)S(1)} %fusion.40), channel_id=1, replica_groups=mesh['com'=8,'arc'=4] {'com'}, dimensions={0} | all-to-all | bytes 4194304 | tf_op jit(solution)/shard_map/all_to_all | solution.py:67
  936.6 7.5 fusion
  944.0 7.5 fusion.8
  954.2 4.0 subtract_bitcast_fusion
  968.2 141.8 %all-gather.11.cloned.1.call-done = f32[4,32,16384]{2,1,0:T(8,128)} async-done(((f32[1,32,16384]{2,1,0:T(8,128)}), f32[4,32,16384]{2,1,0:T(8,128)}) %all-gather.11.cloned.1.call-update) | async-done | bytes 8388624 | tf_op jit(solution)/shard_map/all_gather | solution.py:76
  1110.0 5.4 reduce_sum.289
  1115.5 5.2 multiply_add_fusion
  (107 shorter events, 76.0 us)
Async XLA Ops:
  7.2 14.6 %copy-start = (f32[32,16384]{1,0:T(8,128)S(1)}, f32[32,16384]{1,0:T(8,128)}, u32[]{:S(2)}) copy-start(f32[32,16384]{1,0:T(8,128)} %param.12) | copy-start | bytes 6291460
  7.2 2.1 copy-start.15
  9.3 1.3 copy-start.16
  10.6 1.3 copy-start.13
  11.9 9.9 copy-start.9
  11.9 9.9 copy-start.12
  30.9 5.3 copy-start.14
  30.9 5.3 copy-start.17
  30.9 32.0 %all-to-all-start = ((f32[32,128,128]{2,0,1:T(8,128)}), f32[32,128,128]{2,0,1:T(8,128)}, u32[]{:S(2)}, u32[]{:S(2)}) async-start(f32[32,128,128]{2,0,1:T(8,128)} %fusion.33), calls=%async_computation | async-start | bytes 4194304 | tf_op jit(solution)/shard_map/all_to_all | solution.py:61
  62.9 10.6 all-to-all-start.1
  66.3 224.2 %all-gather.5.cloned.1.call-start = ((), (), s32[]{:S(2)}) async-start(), calls=%async_computation.9 | async-start | bytes 10485760 | tf_op jit(solution)/shard_map/all_gather | solution.py:76
  73.5 6.4 copy-start.11
  110.7 1.6 copy-start.10
  112.3 1.3 copy-start.5
  140.8 422.3 %all-gather.7.cloned.1.call-start = ((), (), s32[]{:S(2)}) async-start(), calls=%async_computation.10 | async-start | bytes 10485760 | tf_op jit(solution)/shard_map/all_gather | solution.py:76
  302.0 9.9 copy-start.6
  388.4 1.3 copy-start.3
  417.0 420.4 %all-gather.9.cloned.1.call-start = ((), (), s32[]{:S(2)}) async-start(), calls=%async_computation.11 | async-start | bytes 10485760 | tf_op jit(solution)/shard_map/all_gather | solution.py:76
  572.5 1.4 copy-start.7
  576.4 9.9 copy-start.4
  662.7 1.3 copy-start.1
  691.2 418.8 %all-gather.11.cloned.1.call-start = ((), (), s32[]{:S(2)}) async-start(), calls=%async_computation.12 | async-start | bytes 10485760 | tf_op jit(solution)/shard_map/all_gather | solution.py:76
  848.8 9.9 copy-start.2
  934.4 1.3 copy-start.8
Sparse Core Ops, SparseCore 0:
  140.9 149.5 all-gather.4
  417.1 145.9 all-gather.6
  691.3 145.9 all-gather.8
  964.0 145.9 all-gather.10
